TPU v7x, 128 devices: a whole 4x4x4 slice. The times are simulated.
128 devices in a mesh: var: 16 (over x, y), samp: 8 (over z, core).
Axes of the slice: x: 4, y: 4, z: 4, core: 2. Of those that a mesh axis runs over, the one named last changes fastest.
Arguments:
- dosage: int32 [24576, 8192], P('samp', 'var'), may hold values from 0 to 2, as said below
- phenotype: float32 [24576], P('samp'), may hold values from -6 to 6
- perm_index: int32 [1024, 24576], P('var', 'samp'), may hold values from 0 to 24575, each once within a row
- seg_lengths: int32 [128], replicated, may hold values from 1 to 128, 8192 in all
Outputs:
- zscore: float32 [1024, 8192], P('samp', 'var')
- thresholds: float32 [1024, 128], P('samp')
Inputs may be any that keep to these rules, and one draw needn't show every extreme that they name: `dosage`: each entry is an allele count. `perm_index`: each row is a permutation of the 24576 sample numbers. `seg_lengths`: the lengths sum to 8192, one of them equals 128.
All inputs are finite; a program needn't handle non-finite values.
Results may differ from a plain program's by a relative error of at most 0.0039.
Values may be sent and summed in bfloat16 or wider, within the bound.
No kernel may reach another device: no remote copies, remote signals or barrier semaphores. Data moves between devices by JAX's collectives and lax.ppermute only.
A program may use at most 64 MiB of HBM per device.

v0:
```python
import math
import jax
import jax.numpy as jnp
from jax import lax
from jax.sharding import PartitionSpec as P

epsilon = 1e-05


def in_order(blocks, dim):
    blocks = jnp.moveaxis(blocks, 0, dim)
    shape = blocks.shape
    return blocks.reshape(*shape[:dim], shape[dim] * shape[dim + 1], *shape[dim + 2 :])


def sent_to_all(value, axis):
    count = lax.axis_size(axis)
    return lax.all_to_all(
        jnp.broadcast_to(value[None], (count, *value.shape)), axis, 0, 0, tiled=True
    )


def collect(value, axis, dim):
    return in_order(sent_to_all(value, axis), dim)


def taken_together(value, axis):
    return sent_to_all(value, axis).sum(axis=0)


def packed_total(arrays, axis):
    ends = [0]
    for a in arrays:
        ends.append(ends[-1] + a.size)
    subtotal = taken_together(jnp.concatenate([a.ravel() for a in arrays]), axis)
    return tuple((subtotal[b:e].reshape(a.shape) for a, b, e in zip(arrays, ends, ends[1:])))


def cut_along(value, dim, count):
    before, after = (value.shape[:dim], value.shape[dim + 1 :])
    return jnp.moveaxis(value.reshape(*before, count, -1, *after), dim, 0)


def sum_at_owner(value, axis, dim):
    count = lax.axis_size(axis)
    blocks = lax.all_to_all(cut_along(value, dim, count), axis, 0, 0, tiled=True)
    return jnp.sum(blocks, axis=0)


def of_everyone(value, axis):
    return sent_to_all(value, axis).max(axis=0)


def pick_traits(rounded, perm_index):
    count_all = rounded.shape[0]
    low_width = math.gcd(128, count_all)
    high_count = count_all // low_width
    table = rounded.reshape(high_count, low_width)
    flat_index = perm_index.reshape(-1)
    entries = flat_index.shape[0]
    block_size = math.gcd(entries, 16384)
    blocks = flat_index.reshape(entries // block_size, block_size)

    def one_block(index_block):
        high_part = index_block // low_width
        low_part = index_block % low_width
        high_iota = lax.broadcasted_iota(jnp.int32, (block_size, high_count), 1)
        selector = (high_part[:, None] == high_iota).astype(jnp.bfloat16)
        table_rows = jnp.dot(selector, table, preferred_element_type=jnp.float32)
        low_iota = lax.broadcasted_iota(jnp.int32, (block_size, low_width), 1)
        chosen = jnp.sum(jnp.where(low_part[:, None] == low_iota, table_rows, 0.0), axis=1)
        return chosen.astype(jnp.bfloat16)

    picked_all = lax.map(one_block, blocks)
    return picked_all.reshape(perm_index.shape)


def running_max(values):
    width = values.shape[1]
    offset = 1
    while offset < width:
        shifted = jnp.pad(values[:, : width - offset], ((0, 0), (offset, 0)))
        values = jnp.maximum(values, shifted)
        offset = offset * 2
    return values


def per_device(dosage, phenotype, perm_index, seg_lengths):
    pheno_all = collect(phenotype, "samp", 0)
    count_all = pheno_all.shape[0]
    centered = pheno_all - jnp.mean(pheno_all)
    pheno_var = jnp.mean(centered * centered)
    rounded = centered.astype(jnp.bfloat16)
    permuted = pick_traits(rounded, perm_index)
    allele_sum, allele_sq = packed_total(
        (
            jnp.sum(dosage, axis=0).astype(jnp.float32),
            jnp.sum(dosage * dosage, axis=0).astype(jnp.float32),
        ),
        "samp",
    )
    allele_var = allele_sq / count_all - (allele_sum / count_all) ** 2
    dosage_bf = dosage.astype(jnp.bfloat16)
    all_perms = lax.all_gather(permuted, "var", axis=0, tiled=True)
    score = sum_at_owner(
        jnp.dot(all_perms, dosage_bf, preferred_element_type=jnp.float32), "samp", 0
    )
    divisor = jnp.sqrt(count_all * (pheno_var + epsilon) * (allele_var + epsilon))
    zscore = score / divisor[None, :]
    local_prefix = running_max(jnp.abs(zscore))
    block_max = local_prefix[:, -1]
    block_maxima = collect(block_max[None, :], "var", 0)
    position = lax.broadcasted_iota(jnp.int32, block_maxima.shape, 0)
    before = jnp.max(jnp.where(position < lax.axis_index("var"), block_maxima, 0.0), axis=0)
    prefix = jnp.maximum(local_prefix, before[:, None])
    width = dosage.shape[1]
    segment_end = jnp.cumsum(seg_lengths) - 1
    local_end = segment_end - lax.axis_index("var") * width
    column_iota = lax.broadcasted_iota(jnp.int32, (width, local_end.shape[0]), 0)
    match = column_iota == local_end[None, :]
    picked = jnp.max(jnp.where(match[None, :, :], prefix[:, :, None], 0.0), axis=1)
    thresholds = of_everyone(picked, "var")
    return (zscore, thresholds)


def solution(mesh):
    return jax.shard_map(
        per_device,
        mesh=mesh,
        in_specs=(P("samp", "var"), P("samp"), P("var", "samp"), P()),
        out_specs=(P("samp", "var"), P("samp", None)),
        check_vma=False,
    )
```

profile of v0, /device:TPU:0, one launch (start us, length us, event | category | flops | bytes accessed | tf_op | source)
XLA Modules:
  0.0 239.6 jit_solution(4275792382053469606)
XLA Ops:
  7.2 1.4 broadcast_in_dim.69
  8.6 5.4 %all-to-all-start = ((f32[8,1,3072]{2,1,0:T(1,128)}), f32[8,1,3072]{2,1,0:T(1,128)S(1)}, u32[]{:S(2)}, u32[]{:S(2)}) async-start(f32[8,1,3072]{2,1,0:T(1,128)} %broadcast_in_dim.69), calls=%async_computation | async-start | bytes 196608 | tf_op jit(solution)/shard_map/all_to_all | solution.py:18
  14.0 1.5 reshape_reshape.3
  15.5 4.3 %all-to-all-done = f32[8,1,3072]{2,1,0:T(1,128)S(1)} async-done(((f32[8,1,3072]{2,1,0:T(1,128)}), f32[8,1,3072]{2,1,0:T(1,128)S(1)}, u32[]{:S(2)}, u32[]{:S(2)}) %all-to-all-start) | async-done | bytes 98336 | tf_op jit(solution)/shard_map/all_to_all | solution.py:18
  19.8 0.8 reduce_sum.66
  21.2 0.3 convert_reduce_fusion
  21.5 62.9 %while.12 = (s32[]{:T(128)}, bf16[12,16384]{1,0:T(8,128)(2,1)S(1)}, s32[12,16384]{1,0:T(8,128)S(1)}, bf16[192,128]{1,0:T(8,128)(2,1)S(1)}, s32[]{:T(128)}, /*index=5*/s32[]{:T(128)}) while((s32[]{:T(128)}, bf16[12,16384]{1,0:T(8,128)(2,1)S(1)}, s32[12,16384]{1,0:T(8,128)S(1)}, bf16[192,128]{1,0:T(8,128)(2,1)S(1)}, s32[]{:T(128)}, ...), condition=%wide.region_3.4_spmd, body=%wide.region_1.3_spmd.sunk | while | flops 815038464 | bytes 671821 | solution.py:74
  21.6 0.1 add_select_fusion.3
  21.7 3.9 %fusion.13 = bf16[16384]{0:T(1024)(128)(2,1)S(1)} fusion(bf16[192,128]{1,0:T(8,128)(2,1)S(1)} %get-tuple-element.117, s32[16384]{0:T(1024)S(1)} %get-tuple-element.100, s32[16384]{0:T(1024)S(1)} %get-tuple-element.101), kind=kOutput, calls=%fused_computation.4.clone.1 | convolution fusion | flops 814727168 | bytes 212992 | tf_op jit(solution)/shard_map/while/body/eval_jaxpr/dot_general | solution.py:69
  25.6 1.1 dynamic_update_slice.8
  26.9 3.9 %fusion.13 = bf16[16384]{0:T(1024)(128)(2,1)S(1)} fusion(bf16[192,128]{1,0:T(8,128)(2,1)S(1)} %get-tuple-element.117, s32[16384]{0:T(1024)S(1)} %get-tuple-element.100, s32[16384]{0:T(1024)S(1)} %get-tuple-element.101), kind=kOutput, calls=%fused_computation.4.clone.1 | convolution fusion | flops 814727168 | bytes 212992 | tf_op jit(solution)/shard_map/while/body/eval_jaxpr/dot_general | solution.py:69
  30.9 1.1 dynamic_update_slice.8
  32.1 0.1 add_select_fusion.3
  32.2 3.9 %fusion.13 = bf16[16384]{0:T(1024)(128)(2,1)S(1)} fusion(bf16[192,128]{1,0:T(8,128)(2,1)S(1)} %get-tuple-element.117, s32[16384]{0:T(1024)S(1)} %get-tuple-element.100, s32[16384]{0:T(1024)S(1)} %get-tuple-element.101), kind=kOutput, calls=%fused_computation.4.clone.1 | convolution fusion | flops 814727168 | bytes 212992 | tf_op jit(solution)/shard_map/while/body/eval_jaxpr/dot_general | solution.py:69
  36.1 1.1 dynamic_update_slice.8
  37.3 0.1 add_select_fusion.3
  37.4 3.9 %fusion.13 = bf16[16384]{0:T(1024)(128)(2,1)S(1)} fusion(bf16[192,128]{1,0:T(8,128)(2,1)S(1)} %get-tuple-element.117, s32[16384]{0:T(1024)S(1)} %get-tuple-element.100, s32[16384]{0:T(1024)S(1)} %get-tuple-element.101), kind=kOutput, calls=%fused_computation.4.clone.1 | convolution fusion | flops 814727168 | bytes 212992 | tf_op jit(solution)/shard_map/while/body/eval_jaxpr/dot_general | solution.py:69
  41.3 1.1 dynamic_update_slice.8
  42.6 3.9 %fusion.13 = bf16[16384]{0:T(1024)(128)(2,1)S(1)} fusion(bf16[192,128]{1,0:T(8,128)(2,1)S(1)} %get-tuple-element.117, s32[16384]{0:T(1024)S(1)} %get-tuple-element.100, s32[16384]{0:T(1024)S(1)} %get-tuple-element.101), kind=kOutput, calls=%fused_computation.4.clone.1 | convolution fusion | flops 814727168 | bytes 212992 | tf_op jit(solution)/shard_map/while/body/eval_jaxpr/dot_general | solution.py:69
  46.6 1.1 dynamic_update_slice.8
  47.9 3.9 %fusion.13 = bf16[16384]{0:T(1024)(128)(2,1)S(1)} fusion(bf16[192,128]{1,0:T(8,128)(2,1)S(1)} %get-tuple-element.117, s32[16384]{0:T(1024)S(1)} %get-tuple-element.100, s32[16384]{0:T(1024)S(1)} %get-tuple-element.101), kind=kOutput, calls=%fused_computation.4.clone.1 | convolution fusion | flops 814727168 | bytes 212992 | tf_op jit(solution)/shard_map/while/body/eval_jaxpr/dot_general | solution.py:69
  51.8 1.1 dynamic_update_slice.8
  53.1 3.9 %fusion.13 = bf16[16384]{0:T(1024)(128)(2,1)S(1)} fusion(bf16[192,128]{1,0:T(8,128)(2,1)S(1)} %get-tuple-element.117, s32[16384]{0:T(1024)S(1)} %get-tuple-element.100, s32[16384]{0:T(1024)S(1)} %get-tuple-element.101), kind=kOutput, calls=%fused_computation.4.clone.1 | convolution fusion | flops 814727168 | bytes 212992 | tf_op jit(solution)/shard_map/while/body/eval_jaxpr/dot_general | solution.py:69
  57.1 1.1 dynamic_update_slice.8
  58.3 3.9 %fusion.13 = bf16[16384]{0:T(1024)(128)(2,1)S(1)} fusion(bf16[192,128]{1,0:T(8,128)(2,1)S(1)} %get-tuple-element.117, s32[16384]{0:T(1024)S(1)} %get-tuple-element.100, s32[16384]{0:T(1024)S(1)} %get-tuple-element.101), kind=kOutput, calls=%fused_computation.4.clone.1 | convolution fusion | flops 814727168 | bytes 212992 | tf_op jit(solution)/shard_map/while/body/eval_jaxpr/dot_general | solution.py:69
  62.3 1.1 dynamic_update_slice.8
  63.6 3.9 %fusion.13 = bf16[16384]{0:T(1024)(128)(2,1)S(1)} fusion(bf16[192,128]{1,0:T(8,128)(2,1)S(1)} %get-tuple-element.117, s32[16384]{0:T(1024)S(1)} %get-tuple-element.100, s32[16384]{0:T(1024)S(1)} %get-tuple-element.101), kind=kOutput, calls=%fused_computation.4.clone.1 | convolution fusion | flops 814727168 | bytes 212992 | tf_op jit(solution)/shard_map/while/body/eval_jaxpr/dot_general | solution.py:69
  67.5 1.1 dynamic_update_slice.8
  68.8 3.9 %fusion.13 = bf16[16384]{0:T(1024)(128)(2,1)S(1)} fusion(bf16[192,128]{1,0:T(8,128)(2,1)S(1)} %get-tuple-element.117, s32[16384]{0:T(1024)S(1)} %get-tuple-element.100, s32[16384]{0:T(1024)S(1)} %get-tuple-element.101), kind=kOutput, calls=%fused_computation.4.clone.1 | convolution fusion | flops 814727168 | bytes 212992 | tf_op jit(solution)/shard_map/while/body/eval_jaxpr/dot_general | solution.py:69
  72.8 1.1 dynamic_update_slice.8
  74.1 3.9 %fusion.13 = bf16[16384]{0:T(1024)(128)(2,1)S(1)} fusion(bf16[192,128]{1,0:T(8,128)(2,1)S(1)} %get-tuple-element.117, s32[16384]{0:T(1024)S(1)} %get-tuple-element.100, s32[16384]{0:T(1024)S(1)} %get-tuple-element.101), kind=kOutput, calls=%fused_computation.4.clone.1 | convolution fusion | flops 814727168 | bytes 212992 | tf_op jit(solution)/shard_map/while/body/eval_jaxpr/dot_general | solution.py:69
  78.0 1.1 dynamic_update_slice.8
  79.3 3.9 %fusion.13 = bf16[16384]{0:T(1024)(128)(2,1)S(1)} fusion(bf16[192,128]{1,0:T(8,128)(2,1)S(1)} %get-tuple-element.117, s32[16384]{0:T(1024)S(1)} %get-tuple-element.100, s32[16384]{0:T(1024)S(1)} %get-tuple-element.101), kind=kOutput, calls=%fused_computation.4.clone.1 | convolution fusion | flops 814727168 | bytes 212992 | tf_op jit(solution)/shard_map/while/body/eval_jaxpr/dot_general | solution.py:69
  83.2 1.1 dynamic_update_slice.8
  84.4 1.3 reshape.151
  85.8 3.5 %fusion.6 = (s32[512]{0:T(512)S(1)}, s32[512]{0:T(512)S(1)}) fusion(s32[3072,512]{1,0:T(8,128)} %param.6), kind=kLoop, calls=%fused_computation.38 | loop fusion | flops 4717568 | bytes 6295552 | tf_op jit(solution)/shard_map/reduce_sum | solution.py:97
  89.3 0.6 broadcast_in_dim.70
  90.0 3.3 %all-to-all-start.2 = ((f32[8,1,1024]{2,1,0:T(1,128)}), f32[8,1,1024]{2,1,0:T(1,128)S(1)}, u32[]{:S(2)}, u32[]{:S(2)}) async-start(f32[8,1,1024]{2,1,0:T(1,128)} %broadcast_in_dim.70), calls=%async_computation.2 | async-start | bytes 65536 | tf_op jit(solution)/shard_map/all_to_all | solution.py:18
  93.3 53.3 %all-gather.2.cloned.1.call-done = bf16[1024,3072]{1,0:T(8,128)(2,1)} async-done(((bf16[64,3072]{1,0:T(8,128)(2,1)}), bf16[1024,3072]{1,0:T(8,128)(2,1)}) %all-gather.2.cloned.1.call-update) | async-done | bytes 6291472 | tf_op jit(solution)/shard_map/all_gather | solution.py:104
  146.6 9.4 %fusion.4 = f32[1024,512]{1,0:T(8,128)} fusion(bf16[1024,3072]{1,0:T(8,128)(2,1)} %all-gather.2.cloned.1.call-done, s32[3072,512]{1,0:T(8,128)} %param.6), kind=kOutput, calls=%fused_computation.16 | convolution fusion | flops 3222798336 | bytes 14680064 | tf_op jit(solution)/shard_map/dot_general | solution.py:106
  155.9 4.4 %all-to-all-start.1 = ((f32[8,128,512]{2,1,0:T(8,128)}), f32[8,128,512]{2,1,0:T(8,128)S(1)}, u32[]{:S(2)}, u32[]{:S(2)}) async-start(f32[8,128,512]{2,1,0:T(8,128)} %bitcast.24), calls=%async_computation.1 | async-start | bytes 4194304 | tf_op jit(solution)/shard_map/all_to_all | solution.py:46
  160.4 0.1 copy.12
  160.5 0.2 reduce-window.8
  160.6 0.1 subtract_reduce_fusion
  160.9 0.8 multiply_reduce_fusion.1
  162.3 25.2 %all-to-all-done.1 = f32[8,128,512]{2,1,0:T(8,128)S(1)} async-done(((f32[8,128,512]{2,1,0:T(8,128)}), f32[8,128,512]{2,1,0:T(8,128)S(1)}, u32[]{:S(2)}, u32[]{:S(2)}) %all-to-all-start.1) | async-done | bytes 2097184 | tf_op jit(solution)/shard_map/all_to_all | solution.py:46
  187.5 0.2 reduce_sum.67
  187.8 0.1 pad_maximum_fusion.8
  188.0 0.1 pad_maximum_fusion.7
  188.1 0.1 pad_maximum_fusion.6
  188.2 0.1 pad_maximum_fusion.5
  188.4 0.1 pad_maximum_fusion.4
  188.5 0.1 pad_maximum_fusion.3
  188.7 0.1 pad_maximum_fusion.2
  188.9 0.2 slice_reduce_fusion
  189.1 0.6 broadcast_in_dim.73
  189.7 5.3 %all-to-all-start.3 = ((f32[16,1,128]{2,1,0:T(1,128)}), f32[16,1,128]{2,1,0:T(1,128)S(1)}, u32[]{:S(2)}, u32[]{:S(2)}) async-start(f32[16,1,128]{2,1,0:T(1,128)} %broadcast_in_dim.73), calls=%async_computation.3 | async-start | bytes 16384 | tf_op jit(solution)/shard_map/all_to_all | solution.py:18
  195.0 7.5 %all-to-all-done.3 = f32[16,1,128]{2,1,0:T(1,128)S(1)} async-done(((f32[16,1,128]{2,1,0:T(1,128)}), f32[16,1,128]{2,1,0:T(1,128)S(1)}, u32[]{:S(2)}, u32[]{:S(2)}) %all-to-all-start.3) | async-done | bytes 8224 | tf_op jit(solution)/shard_map/all_to_all | solution.py:18
  202.5 0.1 select_reduce_fusion.1
  202.6 0.1 broadcast_maximum_fusion
  202.7 10.9 %select_reduce_fusion = f32[128,128]{1,0:T(8,128)S(1)} fusion(f32[128,512]{1,0:T(8,128)S(1)} %broadcast_maximum_fusion, pred[512,128]{1,0:T(8,128)(4,1)S(1)} %iota_compare_fusion.5), kind=kLoop, calls=%fused_computation.14 | loop fusion | flops 16760832 | bytes 393216 | tf_op jit(solution)/shard_map/reduce_max | solution.py:121
  213.6 0.1 broadcast_in_dim.77
  213.7 18.4 %all_to_all.27 = f32[16,128,128]{2,1,0:T(8,128)S(1)} all-to-all(f32[16,128,128]{2,1,0:T(8,128)S(1)} %broadcast_in_dim.77), channel_id=1, replica_groups=mesh['var'=16,'samp'=8] {'var'}, dimensions={0} | all-to-all | bytes 2097152 | tf_op jit(solution)/shard_map/all_to_all | solution.py:18
  232.1 0.7 reduce_max.29
  (54 shorter events, 2.0 us)
Async XLA Ops:
  8.6 11.2 %all-to-all-start = ((f32[8,1,3072]{2,1,0:T(1,128)}), f32[8,1,3072]{2,1,0:T(1,128)S(1)}, u32[]{:S(2)}, u32[]{:S(2)}) async-start(f32[8,1,3072]{2,1,0:T(1,128)} %broadcast_in_dim.69), calls=%async_computation | async-start | bytes 196608 | tf_op jit(solution)/shard_map/all_to_all | solution.py:18
  14.0 132.6 %all-gather.2.cloned.1.call-start = ((), (), s32[]{:S(2)}) async-start(), calls=%async_computation.5 | async-start | bytes 6684672 | tf_op jit(solution)/shard_map/all_gather | solution.py:104
  90.0 66.0 %all-to-all-start.2 = ((f32[8,1,1024]{2,1,0:T(1,128)}), f32[8,1,1024]{2,1,0:T(1,128)S(1)}, u32[]{:S(2)}, u32[]{:S(2)}) async-start(f32[8,1,1024]{2,1,0:T(1,128)} %broadcast_in_dim.70), calls=%async_computation.2 | async-start | bytes 65536 | tf_op jit(solution)/shard_map/all_to_all | solution.py:18
  93.3 67.1 %copy-start.1 = (s32[128]{0:T(128)S(1)}, s32[128]{0:T(128)}, u32[]{:S(2)}) copy-start(s32[128]{0:T(128)} %param.9) | copy-start | bytes 1540
  155.9 31.6 %all-to-all-start.1 = ((f32[8,128,512]{2,1,0:T(8,128)}), f32[8,128,512]{2,1,0:T(8,128)S(1)}, u32[]{:S(2)}, u32[]{:S(2)}) async-start(f32[8,128,512]{2,1,0:T(8,128)} %bitcast.24), calls=%async_computation.1 | async-start | bytes 4194304 | tf_op jit(solution)/shard_map/all_to_all | solution.py:46
  187.8 45.0 %copy-start = (f32[128,512]{1,0:T(8,128)}, f32[128,512]{1,0:T(8,128)S(1)}, u32[]{:S(2)}) copy-start(f32[128,512]{1,0:T(8,128)S(1)} %get-tuple-element.70) | copy-start | bytes 786436
  189.7 12.8 %all-to-all-start.3 = ((f32[16,1,128]{2,1,0:T(1,128)}), f32[16,1,128]{2,1,0:T(1,128)S(1)}, u32[]{:S(2)}, u32[]{:S(2)}) async-start(f32[16,1,128]{2,1,0:T(1,128)} %broadcast_in_dim.73), calls=%async_computation.3 | async-start | bytes 16384 | tf_op jit(solution)/shard_map/all_to_all | solution.py:18
Sparse Core Ops, SparseCore 0:
  85.9 60.6 all-gather.1
where the time goes:
time: 240 us
  waiting for transfers between devices  90.2 us (38%)
  matrix products  56.2 us (23%)
  local copies, waits for them, and re-layouts  20.6 us (9%)
  other arithmetic  19.6 us (8%)
  starting transfers between devices  18.5 us (8%)
  blocking collectives  18.4 us (8%)
  between operations  15.6 us (6%)
    all_gather x1, waiting for transfers between devices, per_device(): all_perms = lax.all_gather(permuted, 'var', axis=0, tiled=True)  53.3 us
    dot_general x12, matrix products, one_block(): table_rows = jnp.dot(selector, table, preferred_element_type=jnp.float32)  46.8 us
    all_to_all x1, waiting for transfers between devices, sum_at_owner(): lax.all_to_all(cut_along(value, dim, count), axis, 0, 0, tiled=True)  25.2 us
    all_to_all x1, blocking collectives, sent_to_all(): lax.all_to_all(jnp.broadcast_to(value[None], (count, *value.shape)), axis...  18.4 us
    all_to_all x3, starting transfers between devices, sent_to_all(): lax.all_to_all(jnp.broadcast_to(value[None], (count, *value.shape)), axis...  14 us
    dynamic_update_slice x12, local copies, waits for them, and re-layouts, pick_traits(): picked_all = lax.map(one_block, blocks)  13.7 us
    all_to_all x3, waiting for transfers between devices, sent_to_all(): lax.all_to_all(jnp.broadcast_to(value[None], (count, *value.shape)), axis...  11.8 us
    reduce_max x1, other arithmetic, per_device(): jnp.max(jnp.where(match[None, :, :], prefix[:, :, None], 0.0), axis=1)  10.9 us
  transfers between devices with their start and end apart: 5, of which 4 were waited for; matrix products, arithmetic and copies ran while one was open for 7% of the time, Pallas kernels for 0%

commit v1 on v0

--- a/solution.py
+++ b/solution.py
@@ -5,6 +5,19 @@
 from jax.sharding import PartitionSpec as P
 
 epsilon = 1e-05
+
+
+def ring_gather(x, axis, dim):
+    ways = lax.axis_size(axis)
+    up = [(d, (d + 1) % ways) for d in range(ways)]
+    down = [(d, (d - 1) % ways) for d in range(ways)]
+    earlier, later = ([x], [x])
+    for _ in range(ways // 2):
+        earlier.append(lax.ppermute(earlier[-1], axis, up))
+    for _ in range((ways - 1) // 2):
+        later.append(lax.ppermute(later[-1], axis, down))
+    line = jnp.concatenate([*earlier[::-1], *later[1:]], axis=dim)
+    return jnp.roll(line, (lax.axis_index(axis) - ways // 2) * x.shape[dim], axis=dim)
 
 
 def in_order(blocks, dim):
@@ -101,7 +114,7 @@
     )
     allele_var = allele_sq / count_all - (allele_sum / count_all) ** 2
     dosage_bf = dosage.astype(jnp.bfloat16)
-    all_perms = lax.all_gather(permuted, "var", axis=0, tiled=True)
+    all_perms = ring_gather(permuted, "var", 0)
     score = sum_at_owner(
         jnp.dot(all_perms, dosage_bf, preferred_element_type=jnp.float32), "samp", 0
     )

time: 240 us -> 276 us (1.15)
  starting transfers between devices: 18.5 us -> 60.1 us
  between operations: 15.6 us -> 2.56 us
  local copies, waits for them, and re-layouts: 20.6 us -> 30.8 us
  matrix products: 56.2 us -> 51.6 us
    ppermute x0 -> x15, waiting for transfers between devices: none -> 54.7 us  [the longest x8 52 us: ring_gather(): earlier.append(lax.ppermute(earlier[-1], axis, up))]
    all_gather x1 -> x0, waiting for transfers between devices: 53.3 us -> none  [per_device(): all_perms = lax.all_gather(permuted, 'var', axis=0, tiled=True)]
    ppermute x0 -> x15, starting transfers between devices: none -> 39.2 us  [the longest x7 37.6 us: ring_gather(): later.append(lax.ppermute(later[-1], axis, down))]
    unnamed x4 -> x51, local copies, waits for them, and re-layouts: 0.01 us -> 10.9 us
    dot_general x1, matrix products: 9.36 us -> 4.77 us  [per_device(): jnp.dot(all_perms, dosage_bf, preferred_element_type=jnp.float32)]
  transfers between devices with their start and end apart: 5 -> 19, of which waited for: 4 -> 11; matrix products, arithmetic and copies ran while one was open for 7% -> 8% of each run, Pallas kernels for 0% -> 0%
where the time goes in v1:
time: 276 us; the launch traced here: 275 us
  waiting for transfers between devices  90.9 us (33%)
  starting transfers between devices  60.1 us (22%)
  matrix products  51.6 us (19%)
  local copies, waits for them, and re-layouts  30.8 us (11%)
  other arithmetic  20.4 us (7%)
  blocking collectives  18.4 us (7%)
    ppermute x8, waiting for transfers between devices, ring_gather(): earlier.append(lax.ppermute(earlier[-1], axis, up))  52 us
    dot_general x12, matrix products, one_block(): table_rows = jnp.dot(selector, table, preferred_element_type=jnp.float32)  46.8 us
    ppermute x7, starting transfers between devices, ring_gather(): later.append(lax.ppermute(later[-1], axis, down))  37.6 us
    all_to_all x1, waiting for transfers between devices, sum_at_owner(): lax.all_to_all(cut_along(value, dim, count), axis, 0, 0, tiled=True)  24.4 us
    all_to_all x1, blocking collectives, sent_to_all(): lax.all_to_all(jnp.broadcast_to(value[None], (count, *value.shape)), axis...  18.4 us
    all_to_all x3, starting transfers between devices, sent_to_all(): lax.all_to_all(jnp.broadcast_to(value[None], (count, *value.shape)), axis...  16.5 us
    dynamic_update_slice x12, local copies, waits for them, and re-layouts, pick_traits(): picked_all = lax.map(one_block, blocks)  13.7 us
    all_to_all x3, waiting for transfers between devices, sent_to_all(): lax.all_to_all(jnp.broadcast_to(value[None], (count, *value.shape)), axis...  11.8 us
  transfers between devices with their start and end apart: 19, of which 11 were waited for; matrix products, arithmetic and copies ran while one was open for 8% of the time, Pallas kernels for 0%

profile of v1, /device:TPU:0, one launch (start us, length us, event | category | flops | bytes accessed | tf_op | source)
XLA Modules:
  0.0 275.3 jit_solution(13606035295653352563)
XLA Ops:
  0.6 1.4 broadcast_in_dim.69
  2.0 5.4 %all-to-all-start = ((f32[8,1,3072]{2,1,0:T(1,128)}), f32[8,1,3072]{2,1,0:T(1,128)S(1)}, u32[]{:S(2)}, u32[]{:S(2)}) async-start(f32[8,1,3072]{2,1,0:T(1,128)} %broadcast_in_dim.69), calls=%async_computation | async-start | bytes 196608 | tf_op jit(solution)/shard_map/all_to_all | solution.py:31
  7.5 1.5 reshape_reshape.3
  8.9 4.3 %all-to-all-done = f32[8,1,3072]{2,1,0:T(1,128)S(1)} async-done(((f32[8,1,3072]{2,1,0:T(1,128)}), f32[8,1,3072]{2,1,0:T(1,128)S(1)}, u32[]{:S(2)}, u32[]{:S(2)}) %all-to-all-start) | async-done | bytes 98336 | tf_op jit(solution)/shard_map/all_to_all | solution.py:31
  15.1 62.9 %while.12 = (s32[]{:T(128)}, bf16[12,16384]{1,0:T(8,128)(2,1)S(1)}, s32[12,16384]{1,0:T(8,128)S(1)}, bf16[192,128]{1,0:T(8,128)(2,1)S(1)}, s32[]{:T(128)}, /*index=5*/s32[]{:T(128)}) while((s32[]{:T(128)}, bf16[12,16384]{1,0:T(8,128)(2,1)S(1)}, s32[12,16384]{1,0:T(8,128)S(1)}, bf16[192,128]{1,0:T(8,128)(2,1)S(1)}, s32[]{:T(128)}, ...), condition=%wide.region_3.4_spmd, body=%wide.region_1.3_spmd.sunk | while | flops 815038464 | bytes 671829 | solution.py:87
  15.3 3.9 %fusion.14 = bf16[16384]{0:T(1024)(128)(2,1)S(1)} fusion(bf16[192,128]{1,0:T(8,128)(2,1)S(1)} %get-tuple-element.117, s32[16384]{0:T(1024)S(1)} %get-tuple-element.100, s32[16384]{0:T(1024)S(1)} %get-tuple-element.101), kind=kOutput, calls=%fused_computation.4.clone.1 | convolution fusion | flops 814727168 | bytes 212992 | tf_op jit(solution)/shard_map/while/body/eval_jaxpr/dot_general | solution.py:82
  19.2 1.1 dynamic_update_slice.8
  20.5 3.9 %fusion.14 = bf16[16384]{0:T(1024)(128)(2,1)S(1)} fusion(bf16[192,128]{1,0:T(8,128)(2,1)S(1)} %get-tuple-element.117, s32[16384]{0:T(1024)S(1)} %get-tuple-element.100, s32[16384]{0:T(1024)S(1)} %get-tuple-element.101), kind=kOutput, calls=%fused_computation.4.clone.1 | convolution fusion | flops 814727168 | bytes 212992 | tf_op jit(solution)/shard_map/while/body/eval_jaxpr/dot_general | solution.py:82
  24.5 1.1 dynamic_update_slice.8
  25.8 3.9 %fusion.14 = bf16[16384]{0:T(1024)(128)(2,1)S(1)} fusion(bf16[192,128]{1,0:T(8,128)(2,1)S(1)} %get-tuple-element.117, s32[16384]{0:T(1024)S(1)} %get-tuple-element.100, s32[16384]{0:T(1024)S(1)} %get-tuple-element.101), kind=kOutput, calls=%fused_computation.4.clone.1 | convolution fusion | flops 814727168 | bytes 212992 | tf_op jit(solution)/shard_map/while/body/eval_jaxpr/dot_general | solution.py:82
  29.7 1.1 dynamic_update_slice.8
  31.0 3.9 %fusion.14 = bf16[16384]{0:T(1024)(128)(2,1)S(1)} fusion(bf16[192,128]{1,0:T(8,128)(2,1)S(1)} %get-tuple-element.117, s32[16384]{0:T(1024)S(1)} %get-tuple-element.100, s32[16384]{0:T(1024)S(1)} %get-tuple-element.101), kind=kOutput, calls=%fused_computation.4.clone.1 | convolution fusion | flops 814727168 | bytes 212992 | tf_op jit(solution)/shard_map/while/body/eval_jaxpr/dot_general | solution.py:82
  34.9 1.1 dynamic_update_slice.8
  36.2 3.9 %fusion.14 = bf16[16384]{0:T(1024)(128)(2,1)S(1)} fusion(bf16[192,128]{1,0:T(8,128)(2,1)S(1)} %get-tuple-element.117, s32[16384]{0:T(1024)S(1)} %get-tuple-element.100, s32[16384]{0:T(1024)S(1)} %get-tuple-element.101), kind=kOutput, calls=%fused_computation.4.clone.1 | convolution fusion | flops 814727168 | bytes 212992 | tf_op jit(solution)/shard_map/while/body/eval_jaxpr/dot_general | solution.py:82
  40.2 1.1 dynamic_update_slice.8
  41.5 3.9 %fusion.14 = bf16[16384]{0:T(1024)(128)(2,1)S(1)} fusion(bf16[192,128]{1,0:T(8,128)(2,1)S(1)} %get-tuple-element.117, s32[16384]{0:T(1024)S(1)} %get-tuple-element.100, s32[16384]{0:T(1024)S(1)} %get-tuple-element.101), kind=kOutput, calls=%fused_computation.4.clone.1 | convolution fusion | flops 814727168 | bytes 212992 | tf_op jit(solution)/shard_map/while/body/eval_jaxpr/dot_general | solution.py:82
  45.4 1.1 dynamic_update_slice.8
  46.7 3.9 %fusion.14 = bf16[16384]{0:T(1024)(128)(2,1)S(1)} fusion(bf16[192,128]{1,0:T(8,128)(2,1)S(1)} %get-tuple-element.117, s32[16384]{0:T(1024)S(1)} %get-tuple-element.100, s32[16384]{0:T(1024)S(1)} %get-tuple-element.101), kind=kOutput, calls=%fused_computation.4.clone.1 | convolution fusion | flops 814727168 | bytes 212992 | tf_op jit(solution)/shard_map/while/body/eval_jaxpr/dot_general | solution.py:82
  50.7 1.1 dynamic_update_slice.8
  51.9 3.9 %fusion.14 = bf16[16384]{0:T(1024)(128)(2,1)S(1)} fusion(bf16[192,128]{1,0:T(8,128)(2,1)S(1)} %get-tuple-element.117, s32[16384]{0:T(1024)S(1)} %get-tuple-element.100, s32[16384]{0:T(1024)S(1)} %get-tuple-element.101), kind=kOutput, calls=%fused_computation.4.clone.1 | convolution fusion | flops 814727168 | bytes 212992 | tf_op jit(solution)/shard_map/while/body/eval_jaxpr/dot_general | solution.py:82
  55.9 1.1 dynamic_update_slice.8
  57.2 3.9 %fusion.14 = bf16[16384]{0:T(1024)(128)(2,1)S(1)} fusion(bf16[192,128]{1,0:T(8,128)(2,1)S(1)} %get-tuple-element.117, s32[16384]{0:T(1024)S(1)} %get-tuple-element.100, s32[16384]{0:T(1024)S(1)} %get-tuple-element.101), kind=kOutput, calls=%fused_computation.4.clone.1 | convolution fusion | flops 814727168 | bytes 212992 | tf_op jit(solution)/shard_map/while/body/eval_jaxpr/dot_general | solution.py:82
  61.1 1.1 dynamic_update_slice.8
  62.4 3.9 %fusion.14 = bf16[16384]{0:T(1024)(128)(2,1)S(1)} fusion(bf16[192,128]{1,0:T(8,128)(2,1)S(1)} %get-tuple-element.117, s32[16384]{0:T(1024)S(1)} %get-tuple-element.100, s32[16384]{0:T(1024)S(1)} %get-tuple-element.101), kind=kOutput, calls=%fused_computation.4.clone.1 | convolution fusion | flops 814727168 | bytes 212992 | tf_op jit(solution)/shard_map/while/body/eval_jaxpr/dot_general | solution.py:82
  66.4 1.1 dynamic_update_slice.8
  67.7 3.9 %fusion.14 = bf16[16384]{0:T(1024)(128)(2,1)S(1)} fusion(bf16[192,128]{1,0:T(8,128)(2,1)S(1)} %get-tuple-element.117, s32[16384]{0:T(1024)S(1)} %get-tuple-element.100, s32[16384]{0:T(1024)S(1)} %get-tuple-element.101), kind=kOutput, calls=%fused_computation.4.clone.1 | convolution fusion | flops 814727168 | bytes 212992 | tf_op jit(solution)/shard_map/while/body/eval_jaxpr/dot_general | solution.py:82
  71.6 1.1 dynamic_update_slice.8
  72.9 3.9 %fusion.14 = bf16[16384]{0:T(1024)(128)(2,1)S(1)} fusion(bf16[192,128]{1,0:T(8,128)(2,1)S(1)} %get-tuple-element.117, s32[16384]{0:T(1024)S(1)} %get-tuple-element.100, s32[16384]{0:T(1024)S(1)} %get-tuple-element.101), kind=kOutput, calls=%fused_computation.4.clone.1 | convolution fusion | flops 814727168 | bytes 212992 | tf_op jit(solution)/shard_map/while/body/eval_jaxpr/dot_general | solution.py:82
  76.8 1.1 dynamic_update_slice.8
  78.6 1.6 collective-permute-start
  80.2 12.6 %collective-permute-done = bf16[64,3072]{1,0:T(8,128)(2,1)S(1)} collective-permute-done((bf16[64,3072]{1,0:T(8,128)(2,1)S(1)}, bf16[64,3072]{1,0:T(8,128)(2,1)S(1)}, u32[]{:S(2)}, u32[]{:S(2)}) %collective-permute-start) | collective-permute-done | bytes 393248 | tf_op jit(solution)/shard_map/ppermute | solution.py:16
  92.8 5.3 %collective-permute-start.8 = (bf16[64,3072]{1,0:T(8,128)(2,1)S(1)}, bf16[64,3072]{1,0:T(8,128)(2,1)S(1)}, u32[]{:S(2)}, u32[]{:S(2)}) collective-permute-start(bf16[64,3072]{1,0:T(8,128)(2,1)S(1)} %reshape.151), channel_id=1, source_target_pairs={{0,120},{8,0},{16,8},{24,16},{32,24},{40,32},{48,40},{56,48},{64,5... | collective-permute-start | bytes 1179656 | tf_op jit(solution)/shard_map/ppermute | solution.py:18
  98.2 8.0 %collective-permute-done.1 = bf16[64,3072]{1,0:T(8,128)(2,1)S(1)} collective-permute-done((bf16[64,3072]{1,0:T(8,128)(2,1)S(1)}, bf16[64,3072]{1,0:T(8,128)(2,1)S(1)}, u32[]{:S(2)}, u32[]{:S(2)}) %collective-permute-start.1) | collective-permute-done | bytes 393248 | tf_op jit(solution)/shard_map/ppermute | solution.py:16
  106.1 5.3 %collective-permute-start.9 = (bf16[64,3072]{1,0:T(8,128)(2,1)S(1)}, bf16[64,3072]{1,0:T(8,128)(2,1)S(1)}, u32[]{:S(2)}, u32[]{:S(2)}) collective-permute-start(bf16[64,3072]{1,0:T(8,128)(2,1)S(1)} %collective-permute-done.8), channel_id=1, source_target_pairs={{0,120},{8,0},{16,8},{24,16},{32,24},{40,32},{48,40},{56,48},{64,5... | collective-permute-start | bytes 1179656 | tf_op jit(solution)/shard_map/ppermute | solution.py:18
  111.5 7.1 %collective-permute-done.2 = bf16[64,3072]{1,0:T(8,128)(2,1)S(1)} collective-permute-done((bf16[64,3072]{1,0:T(8,128)(2,1)S(1)}, bf16[64,3072]{1,0:T(8,128)(2,1)S(1)}, u32[]{:S(2)}, u32[]{:S(2)}) %collective-permute-start.2) | collective-permute-done | bytes 393248 | tf_op jit(solution)/shard_map/ppermute | solution.py:16
  118.6 5.3 %collective-permute-start.10 = (bf16[64,3072]{1,0:T(8,128)(2,1)S(1)}, bf16[64,3072]{1,0:T(8,128)(2,1)S(1)}, u32[]{:S(2)}, u32[]{:S(2)}) collective-permute-start(bf16[64,3072]{1,0:T(8,128)(2,1)S(1)} %collective-permute-done.9), channel_id=1, source_target_pairs={{0,120},{8,0},{16,8},{24,16},{32,24},{40,32},{48,40},{56,48},{64,5... | collective-permute-start | bytes 1179656 | tf_op jit(solution)/shard_map/ppermute | solution.py:18
  124.0 6.3 %collective-permute-done.3 = bf16[64,3072]{1,0:T(8,128)(2,1)S(1)} collective-permute-done((bf16[64,3072]{1,0:T(8,128)(2,1)S(1)}, bf16[64,3072]{1,0:T(8,128)(2,1)S(1)}, u32[]{:S(2)}, u32[]{:S(2)}) %collective-permute-start.3) | collective-permute-done | bytes 393248 | tf_op jit(solution)/shard_map/ppermute | solution.py:16
  130.2 5.3 %collective-permute-start.11 = (bf16[64,3072]{1,0:T(8,128)(2,1)S(1)}, bf16[64,3072]{1,0:T(8,128)(2,1)S(1)}, u32[]{:S(2)}, u32[]{:S(2)}) collective-permute-start(bf16[64,3072]{1,0:T(8,128)(2,1)S(1)} %collective-permute-done.10), channel_id=1, source_target_pairs={{0,120},{8,0},{16,8},{24,16},{32,24},{40,32},{48,40},{56,48},{64,5... | collective-permute-start | bytes 1179656 | tf_op jit(solution)/shard_map/ppermute | solution.py:18
  135.6 5.7 %collective-permute-done.4 = bf16[64,3072]{1,0:T(8,128)(2,1)S(1)} collective-permute-done((bf16[64,3072]{1,0:T(8,128)(2,1)S(1)}, bf16[64,3072]{1,0:T(8,128)(2,1)S(1)}, u32[]{:S(2)}, u32[]{:S(2)}) %collective-permute-start.4) | collective-permute-done | bytes 393248 | tf_op jit(solution)/shard_map/ppermute | solution.py:16
  141.3 5.3 %collective-permute-start.12 = (bf16[64,3072]{1,0:T(8,128)(2,1)S(1)}, bf16[64,3072]{1,0:T(8,128)(2,1)}, u32[]{:S(2)}, u32[]{:S(2)}) collective-permute-start(bf16[64,3072]{1,0:T(8,128)(2,1)S(1)} %collective-permute-done.11), channel_id=1, source_target_pairs={{0,120},{8,0},{16,8},{24,16},{32,24},{40,32},{48,40},{56,48},{64,5... | collective-permute-start | bytes 1179656 | tf_op jit(solution)/shard_map/ppermute | solution.py:18
  146.7 5.7 %collective-permute-done.5 = bf16[64,3072]{1,0:T(8,128)(2,1)S(1)} collective-permute-done((bf16[64,3072]{1,0:T(8,128)(2,1)S(1)}, bf16[64,3072]{1,0:T(8,128)(2,1)S(1)}, u32[]{:S(2)}, u32[]{:S(2)}) %collective-permute-start.5) | collective-permute-done | bytes 393248 | tf_op jit(solution)/shard_map/ppermute | solution.py:16
  152.4 5.4 %collective-permute-start.13 = (bf16[64,3072]{1,0:T(8,128)(2,1)}, bf16[64,3072]{1,0:T(8,128)(2,1)}, u32[]{:S(2)}, u32[]{:S(2)}) collective-permute-start(bf16[64,3072]{1,0:T(8,128)(2,1)} %collective-permute-done.12), channel_id=1, source_target_pairs={{0,120},{8,0},{16,8},{24,16},{32,24},{40,32},{48,40},{56,48},{64,5... | collective-permute-start | bytes 1179656 | tf_op jit(solution)/shard_map/ppermute | solution.py:18
  157.9 6.5 %collective-permute-done.6 = bf16[64,3072]{1,0:T(8,128)(2,1)} collective-permute-done((bf16[64,3072]{1,0:T(8,128)(2,1)S(1)}, bf16[64,3072]{1,0:T(8,128)(2,1)}, u32[]{:S(2)}, u32[]{:S(2)}) %collective-permute-start.6) | collective-permute-done | bytes 393248 | tf_op jit(solution)/shard_map/ppermute | solution.py:16
  164.4 3.5 %fusion.8 = (s32[512]{0:T(512)S(1)}, s32[512]{0:T(512)S(1)}) fusion(s32[3072,512]{1,0:T(8,128)} %param.6), kind=kLoop, calls=%fused_computation.72 | loop fusion | flops 4717568 | bytes 6295552 | tf_op jit(solution)/shard_map/reduce_sum | solution.py:110
  168.6 4.0 %all-to-all-start.2 = ((f32[8,1,1024]{2,1,0:T(1,128)}), f32[8,1,1024]{2,1,0:T(1,128)}, u32[]{:S(2)}, u32[]{:S(2)}) async-start(f32[8,1,1024]{2,1,0:T(1,128)} %broadcast_in_dim.70), calls=%async_computation.2 | async-start | bytes 65536 | tf_op jit(solution)/shard_map/all_to_all | solution.py:31
  172.6 5.4 %collective-permute-start.14 = (bf16[64,3072]{1,0:T(8,128)(2,1)}, bf16[64,3072]{1,0:T(8,128)(2,1)S(1)}, u32[]{:S(2)}, u32[]{:S(2)}) collective-permute-start(bf16[64,3072]{1,0:T(8,128)(2,1)} %collective-permute-done.13), channel_id=1, source_target_pairs={{0,120},{8,0},{16,8},{24,16},{32,24},{40,32},{48,40},{56,48},{64,5... | collective-permute-start | bytes 1179656 | tf_op jit(solution)/shard_map/ppermute | solution.py:18
  178.1 1.0 constant_dynamic-update-slice_fusion.31
  179.1 1.0 constant_dynamic-update-slice_fusion.30
  180.1 1.0 constant_dynamic-update-slice_fusion.29
  181.1 1.0 constant_dynamic-update-slice_fusion.28
  182.5 1.0 constant_dynamic-update-slice_fusion.18
  183.5 1.0 constant_dynamic-update-slice_fusion.17
  184.6 2.7 collective-permute-done.14
  187.3 1.0 constant_dynamic-update-slice_fusion.15
  188.3 1.0 constant_dynamic-update-slice_fusion.14
  189.7 1.0 constant_dynamic-update-slice_fusion.2
  190.8 1.0 constant_dynamic-update-slice_fusion.1
  191.9 4.8 %fusion.4 = f32[1024,512]{1,0:T(8,128)} fusion(bf16[2048,3072]{1,0:T(8,128)(2,1)S(1)} %constant_dynamic-update-slice_fusion, s32[]{:T(128)S(6)} %select_n.56, s32[3072,512]{1,0:T(8,128)S(1)} %bitcast.18), kind=kOutput, calls=%fused_computation.16 | convolution fusion | flops 3222798336 | bytes 14680068 | tf_op jit(solution)/shard_map/dot_general | solution.py:119
  196.6 4.4 %all-to-all-start.1 = ((f32[8,128,512]{2,1,0:T(8,128)}), f32[8,128,512]{2,1,0:T(8,128)S(1)}, u32[]{:S(2)}, u32[]{:S(2)}) async-start(f32[8,128,512]{2,1,0:T(8,128)} %bitcast.25), calls=%async_computation.1 | async-start | bytes 4194304 | tf_op jit(solution)/shard_map/all_to_all | solution.py:59
  203.8 24.4 %all-to-all-done.1 = f32[8,128,512]{2,1,0:T(8,128)S(1)} async-done(((f32[8,128,512]{2,1,0:T(8,128)}), f32[8,128,512]{2,1,0:T(8,128)S(1)}, u32[]{:S(2)}, u32[]{:S(2)}) %all-to-all-start.1) | async-done | bytes 2097184 | tf_op jit(solution)/shard_map/all_to_all | solution.py:59
  230.5 7.1 %all-to-all-start.3 = ((f32[16,1,128]{2,1,0:T(1,128)}), f32[16,1,128]{2,1,0:T(1,128)S(1)}, u32[]{:S(2)}, u32[]{:S(2)}) async-start(f32[16,1,128]{2,1,0:T(1,128)} %broadcast_in_dim.73), calls=%async_computation.3 | async-start | bytes 16384 | tf_op jit(solution)/shard_map/all_to_all | solution.py:31
  237.6 7.5 %all-to-all-done.3 = f32[16,1,128]{2,1,0:T(1,128)S(1)} async-done(((f32[16,1,128]{2,1,0:T(1,128)}), f32[16,1,128]{2,1,0:T(1,128)S(1)}, u32[]{:S(2)}, u32[]{:S(2)}) %all-to-all-start.3) | async-done | bytes 8224 | tf_op jit(solution)/shard_map/all_to_all | solution.py:31
  245.2 10.9 %select_reduce_fusion = f32[128,128]{1,0:T(8,128)S(1)} fusion(f32[128,512]{1,0:T(8,128)S(1)} %broadcast_maximum_fusion, pred[512,128]{1,0:T(8,128)(4,1)S(1)} %iota_compare_fusion.5), kind=kLoop, calls=%fused_computation.14 | loop fusion | flops 16760832 | bytes 393216 | tf_op jit(solution)/shard_map/reduce_max | solution.py:134
  256.3 18.4 %all_to_all.27 = f32[16,128,128]{2,1,0:T(8,128)S(1)} all-to-all(f32[16,128,128]{2,1,0:T(8,128)S(1)} %broadcast_in_dim.77), channel_id=1, replica_groups=mesh['var'=16,'samp'=8] {'var'}, dimensions={0} | all-to-all | bytes 2097152 | tf_op jit(solution)/shard_map/all_to_all | solution.py:31
  (130 shorter events, 10.0 us)
Async XLA Ops:
  2.0 11.2 %all-to-all-start = ((f32[8,1,3072]{2,1,0:T(1,128)}), f32[8,1,3072]{2,1,0:T(1,128)S(1)}, u32[]{:S(2)}, u32[]{:S(2)}) async-start(f32[8,1,3072]{2,1,0:T(1,128)} %broadcast_in_dim.69), calls=%async_computation | async-start | bytes 196608 | tf_op jit(solution)/shard_map/all_to_all | solution.py:31
  13.3 1.9 copy-start.4
  78.6 14.2 %collective-permute-start = (bf16[64,3072]{1,0:T(8,128)(2,1)S(1)}, bf16[64,3072]{1,0:T(8,128)(2,1)S(1)}, u32[]{:S(2)}, u32[]{:S(2)}) collective-permute-start(bf16[64,3072]{1,0:T(8,128)(2,1)S(1)} %reshape.151), channel_id=1, source_target_pairs={{0,8},{8,16},{16,24},{24,32},{32,40},{40,48},{48,56},{56,64},{64,7... | collective-permute-start | bytes 1179656 | tf_op jit(solution)/shard_map/ppermute | solution.py:16
  92.8 13.3 %collective-permute-start.1 = (bf16[64,3072]{1,0:T(8,128)(2,1)S(1)}, bf16[64,3072]{1,0:T(8,128)(2,1)S(1)}, u32[]{:S(2)}, u32[]{:S(2)}) collective-permute-start(bf16[64,3072]{1,0:T(8,128)(2,1)S(1)} %collective-permute-done), channel_id=1, source_target_pairs={{0,8},{8,16},{16,24},{24,32},{32,40},{40,48},{48,56},{56,64},{64,7... | collective-permute-start | bytes 1179656 | tf_op jit(solution)/shard_map/ppermute | solution.py:16
  92.8 13.3 %collective-permute-start.8 = (bf16[64,3072]{1,0:T(8,128)(2,1)S(1)}, bf16[64,3072]{1,0:T(8,128)(2,1)S(1)}, u32[]{:S(2)}, u32[]{:S(2)}) collective-permute-start(bf16[64,3072]{1,0:T(8,128)(2,1)S(1)} %reshape.151), channel_id=1, source_target_pairs={{0,120},{8,0},{16,8},{24,16},{32,24},{40,32},{48,40},{56,48},{64,5... | collective-permute-start | bytes 1179656 | tf_op jit(solution)/shard_map/ppermute | solution.py:18
  106.1 12.5 %collective-permute-start.2 = (bf16[64,3072]{1,0:T(8,128)(2,1)S(1)}, bf16[64,3072]{1,0:T(8,128)(2,1)S(1)}, u32[]{:S(2)}, u32[]{:S(2)}) collective-permute-start(bf16[64,3072]{1,0:T(8,128)(2,1)S(1)} %collective-permute-done.1), channel_id=1, source_target_pairs={{0,8},{8,16},{16,24},{24,32},{32,40},{40,48},{48,56},{56,64},{64,7... | collective-permute-start | bytes 1179656 | tf_op jit(solution)/shard_map/ppermute | solution.py:16
  106.1 12.5 %collective-permute-start.9 = (bf16[64,3072]{1,0:T(8,128)(2,1)S(1)}, bf16[64,3072]{1,0:T(8,128)(2,1)S(1)}, u32[]{:S(2)}, u32[]{:S(2)}) collective-permute-start(bf16[64,3072]{1,0:T(8,128)(2,1)S(1)} %collective-permute-done.8), channel_id=1, source_target_pairs={{0,120},{8,0},{16,8},{24,16},{32,24},{40,32},{48,40},{56,48},{64,5... | collective-permute-start | bytes 1179656 | tf_op jit(solution)/shard_map/ppermute | solution.py:18
  118.6 11.6 %collective-permute-start.3 = (bf16[64,3072]{1,0:T(8,128)(2,1)S(1)}, bf16[64,3072]{1,0:T(8,128)(2,1)S(1)}, u32[]{:S(2)}, u32[]{:S(2)}) collective-permute-start(bf16[64,3072]{1,0:T(8,128)(2,1)S(1)} %collective-permute-done.2), channel_id=1, source_target_pairs={{0,8},{8,16},{16,24},{24,32},{32,40},{40,48},{48,56},{56,64},{64,7... | collective-permute-start | bytes 1179656 | tf_op jit(solution)/shard_map/ppermute | solution.py:16
  118.6 11.6 %collective-permute-start.10 = (bf16[64,3072]{1,0:T(8,128)(2,1)S(1)}, bf16[64,3072]{1,0:T(8,128)(2,1)S(1)}, u32[]{:S(2)}, u32[]{:S(2)}) collective-permute-start(bf16[64,3072]{1,0:T(8,128)(2,1)S(1)} %collective-permute-done.9), channel_id=1, source_target_pairs={{0,120},{8,0},{16,8},{24,16},{32,24},{40,32},{48,40},{56,48},{64,5... | collective-permute-start | bytes 1179656 | tf_op jit(solution)/shard_map/ppermute | solution.py:18
  130.2 11.1 %collective-permute-start.4 = (bf16[64,3072]{1,0:T(8,128)(2,1)S(1)}, bf16[64,3072]{1,0:T(8,128)(2,1)S(1)}, u32[]{:S(2)}, u32[]{:S(2)}) collective-permute-start(bf16[64,3072]{1,0:T(8,128)(2,1)S(1)} %collective-permute-done.3), channel_id=1, source_target_pairs={{0,8},{8,16},{16,24},{24,32},{32,40},{40,48},{48,56},{56,64},{64,7... | collective-permute-start | bytes 1179656 | tf_op jit(solution)/shard_map/ppermute | solution.py:16
  130.2 11.1 %collective-permute-start.11 = (bf16[64,3072]{1,0:T(8,128)(2,1)S(1)}, bf16[64,3072]{1,0:T(8,128)(2,1)S(1)}, u32[]{:S(2)}, u32[]{:S(2)}) collective-permute-start(bf16[64,3072]{1,0:T(8,128)(2,1)S(1)} %collective-permute-done.10), channel_id=1, source_target_pairs={{0,120},{8,0},{16,8},{24,16},{32,24},{40,32},{48,40},{56,48},{64,5... | collective-permute-start | bytes 1179656 | tf_op jit(solution)/shard_map/ppermute | solution.py:18
  141.3 11.1 %copy-start = (bf16[64,3072]{1,0:T(8,128)(2,1)}, bf16[64,3072]{1,0:T(8,128)(2,1)S(1)}, u32[]{:S(2)}) copy-start(bf16[64,3072]{1,0:T(8,128)(2,1)S(1)} %collective-permute-done.4) | copy-start | bytes 1179652
  141.3 11.1 %collective-permute-start.5 = (bf16[64,3072]{1,0:T(8,128)(2,1)S(1)}, bf16[64,3072]{1,0:T(8,128)(2,1)S(1)}, u32[]{:S(2)}, u32[]{:S(2)}) collective-permute-start(bf16[64,3072]{1,0:T(8,128)(2,1)S(1)} %collective-permute-done.4), channel_id=1, source_target_pairs={{0,8},{8,16},{16,24},{24,32},{32,40},{40,48},{48,56},{56,64},{64,7... | collective-permute-start | bytes 1179656 | tf_op jit(solution)/shard_map/ppermute | solution.py:16
  141.3 11.1 %collective-permute-start.12 = (bf16[64,3072]{1,0:T(8,128)(2,1)S(1)}, bf16[64,3072]{1,0:T(8,128)(2,1)}, u32[]{:S(2)}, u32[]{:S(2)}) collective-permute-start(bf16[64,3072]{1,0:T(8,128)(2,1)S(1)} %collective-permute-done.11), channel_id=1, source_target_pairs={{0,120},{8,0},{16,8},{24,16},{32,24},{40,32},{48,40},{56,48},{64,5... | collective-permute-start | bytes 1179656 | tf_op jit(solution)/shard_map/ppermute | solution.py:18
  152.4 5.5 %copy-start.2 = (bf16[64,3072]{1,0:T(8,128)(2,1)}, bf16[64,3072]{1,0:T(8,128)(2,1)S(1)}, u32[]{:S(2)}) copy-start(bf16[64,3072]{1,0:T(8,128)(2,1)S(1)} %collective-permute-done.5) | copy-start | bytes 1179652
  152.4 12.0 %collective-permute-start.6 = (bf16[64,3072]{1,0:T(8,128)(2,1)S(1)}, bf16[64,3072]{1,0:T(8,128)(2,1)}, u32[]{:S(2)}, u32[]{:S(2)}) collective-permute-start(bf16[64,3072]{1,0:T(8,128)(2,1)S(1)} %collective-permute-done.5), channel_id=1, source_target_pairs={{0,8},{8,16},{16,24},{24,32},{32,40},{40,48},{48,56},{56,64},{64,7... | collective-permute-start | bytes 1179656 | tf_op jit(solution)/shard_map/ppermute | solution.py:16
  152.4 20.2 %collective-permute-start.13 = (bf16[64,3072]{1,0:T(8,128)(2,1)}, bf16[64,3072]{1,0:T(8,128)(2,1)}, u32[]{:S(2)}, u32[]{:S(2)}) collective-permute-start(bf16[64,3072]{1,0:T(8,128)(2,1)} %collective-permute-done.12), channel_id=1, source_target_pairs={{0,120},{8,0},{16,8},{24,16},{32,24},{40,32},{48,40},{56,48},{64,5... | collective-permute-start | bytes 1179656 | tf_op jit(solution)/shard_map/ppermute | solution.py:18
  164.4 13.6 %collective-permute-start.7 = (bf16[64,3072]{1,0:T(8,128)(2,1)}, bf16[64,3072]{1,0:T(8,128)(2,1)}, u32[]{:S(2)}, u32[]{:S(2)}) collective-permute-start(bf16[64,3072]{1,0:T(8,128)(2,1)} %collective-permute-done.6), channel_id=1, source_target_pairs={{0,8},{8,16},{16,24},{24,32},{32,40},{40,48},{48,56},{56,64},{64,7... | collective-permute-start | bytes 1179656 | tf_op jit(solution)/shard_map/ppermute | solution.py:16
  168.6 28.0 %all-to-all-start.2 = ((f32[8,1,1024]{2,1,0:T(1,128)}), f32[8,1,1024]{2,1,0:T(1,128)}, u32[]{:S(2)}, u32[]{:S(2)}) async-start(f32[8,1,1024]{2,1,0:T(1,128)} %broadcast_in_dim.70), calls=%async_computation.2 | async-start | bytes 65536 | tf_op jit(solution)/shard_map/all_to_all | solution.py:31
  172.6 16.7 %copy-start.3 = (bf16[64,3072]{1,0:T(8,128)(2,1)S(1)}, bf16[64,3072]{1,0:T(8,128)(2,1)}, u32[]{:S(2)}) copy-start(bf16[64,3072]{1,0:T(8,128)(2,1)} %copy-done.2) | copy-start | bytes 1179652
  172.6 16.8 %copy-start.1 = (bf16[64,3072]{1,0:T(8,128)(2,1)S(1)}, bf16[64,3072]{1,0:T(8,128)(2,1)}, u32[]{:S(2)}) copy-start(bf16[64,3072]{1,0:T(8,128)(2,1)} %copy-done) | copy-start | bytes 1179652
  172.6 19.2 %slice-start = ((s8[6291456]{0:T(1024)(128)(4,1)}), s8[4194304]{0:T(1024)(128)(4,1)S(1)}, s32[]{:S(2)}) async-start(s8[6291456]{0:T(1024)(128)(4,1)} %bitcast.17), calls=%async_computation.5 | async-start | bytes 8388608
  172.6 14.6 %collective-permute-start.14 = (bf16[64,3072]{1,0:T(8,128)(2,1)}, bf16[64,3072]{1,0:T(8,128)(2,1)S(1)}, u32[]{:S(2)}, u32[]{:S(2)}) collective-permute-start(bf16[64,3072]{1,0:T(8,128)(2,1)} %collective-permute-done.13), channel_id=1, source_target_pairs={{0,120},{8,0},{16,8},{24,16},{32,24},{40,32},{48,40},{56,48},{64,5... | collective-permute-start | bytes 1179656 | tf_op jit(solution)/shard_map/ppermute | solution.py:18
  184.5 7.3 %slice-start.1 = ((s8[6291456]{0:T(1024)(128)(4,1)}), s8[2097152]{0:T(1024)(128)(4,1)S(1)}, s32[]{:S(2)}) async-start(s8[6291456]{0:T(1024)(128)(4,1)} %bitcast.17), calls=%async_computation.6 | async-start | bytes 4194304
  191.9 9.2 %copy-start.7 = (s32[128]{0:T(128)S(1)}, s32[128]{0:T(128)}, u32[]{:S(2)}) copy-start(s32[128]{0:T(128)} %param.9) | copy-start | bytes 1540
  191.9 10.5 %copy-start.5 = (f32[8,1,3072]{2,1,0:T(1,128)S(1)}, f32[8,1,3072]{2,1,0:T(1,128)}, u32[]{:S(2)}) copy-start(f32[8,1,3072]{2,1,0:T(1,128)} %copy-done.4) | copy-start | bytes 294916
  196.6 31.6 %all-to-all-start.1 = ((f32[8,128,512]{2,1,0:T(8,128)}), f32[8,128,512]{2,1,0:T(8,128)S(1)}, u32[]{:S(2)}, u32[]{:S(2)}) async-start(f32[8,128,512]{2,1,0:T(8,128)} %bitcast.25), calls=%async_computation.1 | async-start | bytes 4194304 | tf_op jit(solution)/shard_map/all_to_all | solution.py:59
  228.5 46.8 %copy-start.6 = (f32[128,512]{1,0:T(8,128)}, f32[128,512]{1,0:T(8,128)S(1)}, u32[]{:S(2)}) copy-start(f32[128,512]{1,0:T(8,128)S(1)} %get-tuple-element.70) | copy-start | bytes 786436
  230.5 14.6 %all-to-all-start.3 = ((f32[16,1,128]{2,1,0:T(1,128)}), f32[16,1,128]{2,1,0:T(1,128)S(1)}, u32[]{:S(2)}, u32[]{:S(2)}) async-start(f32[16,1,128]{2,1,0:T(1,128)} %broadcast_in_dim.73), calls=%async_computation.3 | async-start | bytes 16384 | tf_op jit(solution)/shard_map/all_to_all | solution.py:31
